TPU v7x, 256 devices: a whole 4x4x8 slice. The times are simulated.
256 devices in a mesh: row: 8 (over y, x_hi), col: 32 (over z, x_lo, core).
Axes of the slice: x: 4 (x_hi: 2, x_lo: 2; x = x_hi * 2 + x_lo), y: 4, z: 8, core: 2. Of those that a mesh axis runs over, the one named last changes fastest.
Arguments:
- pair: float32 [512, 512, 128], P('row', 'col'), may hold values from -6 to 6
- in_gain: float32 [2, 128], replicated, may hold values from 1 to 4
- in_bias: float32 [2, 128], replicated, may hold values from -1.5 to 1.5
- proj_weight: bfloat16 [2, 128, 640], replicated, may hold values from -0.5 to 0.5
- proj_bias: float32 [2, 640], replicated, may hold values from -1.5 to 1.5
- mid_gain: float32 [2, 128], replicated, may hold values from 0.5 to 2
- mid_bias: float32 [2, 128], replicated, may hold values from -3 to 3
- out_weight: bfloat16 [2, 128, 128], replicated, may hold values from -0.5 to 0.5
- out_bias: float32 [2, 128], replicated, may hold values from -3 to 3
Outputs:
- updated: float32 [512, 512, 128], P('row', 'col')
All inputs are finite; a program needn't handle non-finite values.
Results may differ from a plain program's by a relative error of at most 0.015.
Values may be sent and summed in bfloat16 or wider, within the bound.
A program may use at most 128 MiB of HBM per device.

v0:
```python
import jax
import jax.numpy as jnp
from jax import lax
from jax.sharding import PartitionSpec as P


def copy_for_each(value, axis):
    peers = lax.axis_size(axis)
    return lax.all_to_all(
        jnp.broadcast_to(value[None], (peers, *value.shape)), axis, 0, 0, tiled=True
    )


def joined_along(blocks, dim):
    blocks = jnp.moveaxis(blocks, 0, dim)
    lengths = blocks.shape
    return blocks.reshape(*lengths[:dim], lengths[dim] * lengths[dim + 1], *lengths[dim + 2 :])


def collect(value, axis, dim):
    blocks = copy_for_each(value, axis)
    return joined_along(blocks, dim)


def split_up(value, dim, peers):
    before, after = (value.shape[:dim], value.shape[dim + 1 :])
    return jnp.moveaxis(value.reshape(*before, peers, -1, *after), dim, 0)


def sent_and_summed(value, axis, dim):
    blocks = split_up(value, dim, lax.axis_size(axis))
    arrived = lax.all_to_all(blocks, axis, split_axis=0, concat_axis=0, tiled=True)
    return arrived.astype(jnp.float32).sum(axis=0)


def layer_norm(values, gain, offset):
    mean = jnp.mean(values, -1, keepdims=True)
    centred = values - mean
    variance = jnp.mean(centred * centred, -1, keepdims=True)
    return centred * lax.rsqrt(variance + 1e-05) * gain + offset


def projections(state, update, in_gain, in_bias, proj_weight, proj_bias):
    hidden = (proj_weight.shape[2] - state.shape[2]) // 4
    normed = layer_norm(state, in_gain[update], in_bias[update]).astype(jnp.bfloat16)
    proj = (
        jnp.dot(normed, proj_weight[update], preferred_element_type=jnp.float32) + proj_bias[update]
    )
    left = (jax.nn.sigmoid(proj[..., hidden : 2 * hidden]) * proj[..., 0:hidden]).astype(
        jnp.bfloat16
    )
    right = (
        jax.nn.sigmoid(proj[..., 3 * hidden : 4 * hidden]) * proj[..., 2 * hidden : 3 * hidden]
    ).astype(jnp.bfloat16)
    gate = jax.nn.sigmoid(proj[..., 4 * hidden :])
    left_major = jnp.transpose(left, (2, 0, 1))
    right_major = jnp.transpose(right, (2, 0, 1))
    return (left_major, right_major, gate)


def finish(state, mixed_major, gate, update, mid_gain, mid_bias, out_weight, out_bias):
    mixed = jnp.transpose(mixed_major, (1, 2, 0))
    middle = layer_norm(mixed, mid_gain[update], mid_bias[update]).astype(jnp.bfloat16)
    outcome = (
        jnp.dot(middle, out_weight[update], preferred_element_type=jnp.float32) + out_bias[update]
    )
    return state + gate * outcome


def body(pair, in_gain, in_bias, proj_weight, proj_bias, mid_gain, mid_bias, out_weight, out_bias):
    left, right, gate = projections(pair, 0, in_gain, in_bias, proj_weight, proj_bias)
    strip = collect(right, "row", 1)
    right_rows = lax.all_to_all(strip, "col", split_axis=1, concat_axis=2, tiled=True)
    mixed = jnp.einsum(
        "cik,cjk->cij",
        lax.all_gather(left, "col", axis=2, tiled=True),
        right_rows,
        preferred_element_type=jnp.float32,
    )
    state = finish(pair, mixed, gate, 0, mid_gain, mid_bias, out_weight, out_bias)
    left, right, gate = projections(state, 1, in_gain, in_bias, proj_weight, proj_bias)
    terms = jnp.einsum(
        "cki,ckj->cij",
        lax.all_gather(left, "col", axis=2, tiled=True),
        right,
        preferred_element_type=jnp.float32,
    )
    mixed = sent_and_summed(terms.astype(jnp.bfloat16), "row", 1)
    return finish(state, mixed, gate, 1, mid_gain, mid_bias, out_weight, out_bias)


def solution(mesh):
    placed = (P("row", "col", None), P(), P(), P(), P(), P(), P(), P(), P())
    return jax.shard_map(
        body, mesh=mesh, in_specs=placed, out_specs=P("row", "col", None), check_vma=False
    )
```

profile of v0, /device:TPU:1, one launch (start us, length us, event | category | flops | bytes accessed | tf_op | source)
XLA Modules:
  0.0 363.5 jit_solution(2842531356005309240)
XLA Ops:
  6.5 1.2 reduce_sum.81
  7.9 1.4 multiply_reduce_fusion.3
  9.5 0.8 slice_reduce_fusion
  10.3 0.8 slice_bitcast_fusion.3
  11.1 1.7 convolution_add_fusion.1
  12.8 1.6 copy-done
  14.4 1.0 fusion.39
  15.4 0.3 broadcast_in_dim.2
  15.6 48.4 %all_to_all.28 = bf16[8,128,64,16]{1,3,2,0:T(8,128)(2,1)} all-to-all(bf16[8,128,64,16]{1,3,2,0:T(8,128)(2,1)S(1)} %broadcast_in_dim.2), channel_id=1, replica_groups=mesh['row'=8,'col'=32] {'row'}, dimensions={0} | all-to-all | bytes 4194304 | tf_op jit(solution)/shard_map/all_to_all | solution.py:9
  64.0 14.7 %all-to-all-start.1 = ((bf16[128,512,16]{0,2,1:T(8,128)(2,1)}), bf16[128,512,16]{0,2,1:T(8,128)(2,1)S(1)}, u32[]{:S(2)}, u32[]{:S(2)}) async-start(bf16[128,512,16]{0,2,1:T(8,128)(2,1)} %bitcast.72), calls=%async_computation.1 | async-start | bytes 4194304 | tf_op jit(solution)/shard_map/all_to_all | solution.py:73
  78.7 0.2 all-gather.5.cloned.1.call-start
  79.0 64.4 %all-to-all-done.1 = bf16[128,512,16]{0,2,1:T(8,128)(2,1)S(1)} async-done(((bf16[128,512,16]{0,2,1:T(8,128)(2,1)}), bf16[128,512,16]{0,2,1:T(8,128)(2,1)S(1)}, u32[]{:S(2)}, u32[]{:S(2)}) %all-to-all-start.1) | async-done | bytes 2097184 | tf_op jit(solution)/shard_map/all_to_all | solution.py:73
  143.4 1.9 copy.54
  145.3 3.4 copy.56
  148.8 29.1 %copy.55 = bf16[128,64,512]{1,2,0:T(8,128)(2,1)} copy(bf16[128,64,512]{0,2,1:T(8,128)(2,1)} %all-gather.3.cloned.1.call-done) | data formatting | bytes 16777216 | tf_op jit(solution)/shard_map/all_gather | solution.py:76
  177.9 7.0 %fusion.50 = (f32[64,16]{0,1:T(8,128)S(1)}, f32[64,16,128]{0,1,2:T(8,128)S(1)}) fusion(bf16[128,16,512]{2,1,0:T(8,128)(2,1)S(1)} %copy.56, bf16[128,64,512]{1,2,0:T(8,128)(2,1)} %copy.55), kind=kOutput, calls=%fused_computation.97 | convolution fusion | flops 134347776 | bytes 11014144 | tf_op jit(solution)/shard_map/cik,cjk->cij/dot_general | solution.py:74
  185.2 0.3 add_convert_fusion
  185.6 0.6 copy.57
  186.2 1.4 fusion.51
  187.8 0.4 multiply_reduce_fusion.2
  188.3 0.6 convolution_add_fusion
  188.9 1.6 copy-done.1
  190.5 1.0 fusion.41
  191.5 0.5 copy.63
  192.1 86.6 %all-gather.5.cloned.1.call-done = bf16[128,64,512]{0,2,1:T(8,128)(2,1)} async-done(((bf16[128,64,16]{0,2,1:T(8,128)(2,1)}), bf16[128,64,512]{0,2,1:T(8,128)(2,1)}) %all-gather.5.cloned.1.call-update) | async-done | bytes 8388624 | tf_op jit(solution)/shard_map/all_gather | solution.py:84
  278.6 29.1 %copy.62 = bf16[128,64,512]{1,2,0:T(8,128)(2,1)} copy(bf16[128,64,512]{0,2,1:T(8,128)(2,1)} %all-gather.5.cloned.1.call-done) | data formatting | bytes 16777216 | tf_op jit(solution)/shard_map/all_gather | solution.py:84
  307.8 8.0 %convolution_convert_fusion = bf16[128,512,16]{1,2,0:T(8,128)(2,1)S(1)} fusion(bf16[128,64,512]{1,2,0:T(8,128)(2,1)} %copy.62, bf16[128,64,16]{1,2,0:T(8,128)(2,1)S(1)} %copy.63), kind=kOutput, calls=%fused_computation.1 | convolution fusion | flops 135266304 | bytes 10747904 | tf_op jit(solution)/shard_map/cki,ckj->cij/dot_general | solution.py:82
  315.8 3.9 %copy.64 = bf16[128,512,16]{0,2,1:T(8,128)(2,1)} copy(bf16[128,512,16]{1,2,0:T(8,128)(2,1)S(1)} %convolution_convert_fusion) | data formatting | bytes 4194304 | tf_op jit(solution)/shard_map/convert_element_type | solution.py:88
  319.8 33.3 %all_to_all.29 = bf16[8,128,64,16]{1,3,2,0:T(8,128)(2,1)S(1)} all-to-all(bf16[8,128,64,16]{1,3,2,0:T(8,128)(2,1)} %bitcast.74), channel_id=1, replica_groups=mesh['row'=8,'col'=32] {'row'}, dimensions={0} | all-to-all | bytes 4194304 | tf_op jit(solution)/shard_map/all_to_all | solution.py:32
  353.1 0.3 convert_reduce_fusion
  353.8 0.4 multiply_reduce_fusion.1
  354.3 2.3 fusion.3
  (42 shorter events, 1.4 us)
Async XLA Ops:
  6.5 142.2 %all-gather.3.cloned.1.call-start = ((), (), s32[]{:S(2)}) async-start(), calls=%async_computation.3 | async-start | bytes 8650752 | tf_op jit(solution)/shard_map/all_gather | solution.py:76
  12.8 1.6 copy-start
  64.0 14.9 %copy-start.4 = (f32[2,128]{1,0:T(2,128)S(1)}, f32[2,128]{1,0:T(2,128)}, u32[]{:S(2)}) copy-start(f32[2,128]{1,0:T(2,128)} %param.17) | copy-start | bytes 3076
  64.0 15.0 %copy-start.5 = (f32[2,128]{1,0:T(2,128)S(1)}, f32[2,128]{1,0:T(2,128)}, u32[]{:S(2)}) copy-start(f32[2,128]{1,0:T(2,128)} %param.15) | copy-start | bytes 3076
  64.0 15.0 %copy-start.6 = (f32[2,128]{1,0:T(2,128)S(1)}, f32[2,128]{1,0:T(2,128)}, u32[]{:S(2)}) copy-start(f32[2,128]{1,0:T(2,128)} %param.14) | copy-start | bytes 3076
  64.0 79.4 %all-to-all-start.1 = ((bf16[128,512,16]{0,2,1:T(8,128)(2,1)}), bf16[128,512,16]{0,2,1:T(8,128)(2,1)S(1)}, u32[]{:S(2)}, u32[]{:S(2)}) async-start(bf16[128,512,16]{0,2,1:T(8,128)(2,1)} %bitcast.72), calls=%async_computation.1 | async-start | bytes 4194304 | tf_op jit(solution)/shard_map/all_to_all | solution.py:73
  78.7 199.9 %all-gather.5.cloned.1.call-start = ((), (), s32[]{:S(2)}) async-start(), calls=%async_computation.4 | async-start | bytes 8650752 | tf_op jit(solution)/shard_map/all_gather | solution.py:84
  185.0 1.2 copy-start.2
  185.0 1.2 copy-start.7
  185.6 2.7 copy-start.3
  188.9 1.6 copy-start.1
Sparse Core Ops, SparseCore 0:
  15.5 130.9 all-gather.2
  191.6 86.9 all-gather.4
where the time goes:
time: 365 us; the launch traced here: 363 us
  waiting for transfers between devices  151 us (41%)
  blocking collectives  81.7 us (22%)
  local copies, waits for them, and re-layouts  74.6 us (20%)
  matrix products  21.1 us (6%)
  starting transfers between devices  14.9 us (4%)
  between operations  13.6 us (4%)
  other arithmetic  6.47 us (2%)
    all_gather x2, waiting for transfers between devices, body(): lax.all_gather(left, 'col', axis=2, tiled=True)  86.6 us
    all_to_all x1, waiting for transfers between devices, body(): lax.all_to_all(strip, 'col', split_axis=1, concat_axis=2, tiled=True)  64.4 us
    all_gather x2, local copies, waits for them, and re-layouts, body(): lax.all_gather(left, 'col', axis=2, tiled=True)  58.3 us
    all_to_all x1, blocking collectives, copy_for_each(): lax.all_to_all(jnp.broadcast_to(value[None], (peers, *value.shape)), axis...  48.4 us
    all_to_all x1, blocking collectives, sent_and_summed(): lax.all_to_all(blocks, axis, split_axis=0, concat_axis=0, tiled=True)  33.3 us
    all_to_all x1, starting transfers between devices, body(): lax.all_to_all(strip, 'col', split_axis=1, concat_axis=2, tiled=True)  14.7 us
    dot_general x1, matrix products, body(): jnp.einsum('cki,ckj->cij', lax.all_gather(left, 'col', axis=2, tiled=True...  8.04 us
  transfers between devices with their start and end apart: 3, of which 2 were waited for; matrix products, arithmetic and copies ran while one was open for 2% of the time, Pallas kernels for 0%

commit v1 on v0

v1 whole, which is shorter than its diff:
```python
import functools

import jax
import jax.numpy as jnp
from jax import lax
from jax.experimental import pallas as pl
from jax.experimental.pallas import tpu as pltpu
from jax.sharding import PartitionSpec as P

MESH = pl.DeviceIdType.MESH
F32 = jnp.float32
BF16 = jnp.bfloat16
EPS = 1e-05


def norm_rows(values, gain, offset):
    mean = jnp.mean(values, -1, keepdims=True)
    centred = values - mean
    variance = jnp.mean(centred * centred, -1, keepdims=True)
    return centred * lax.rsqrt(variance + EPS) * gain + offset


def kernel(
    pair_ref, in_gain, in_bias, proj_w, proj_b, mid_gain, mid_bias, out_w, out_b,
    out_ref,
    w_t, bias_t, mgain_t, mbias_t,
    state, gates, tmp_l, tmp_r,
    send_l, send_r, send_m, recv_l, recv_r, recv_m,
    a_l0, a_l1, a_r, mixed,
    sems_send, sems_recv, sem_enter,
):
    row = lax.axis_index("row")
    col = lax.axis_index("col")
    y, xh = lax.div(row, 2), lax.rem(row, 2)
    z, low = lax.div(col, 4), lax.rem(col, 4)
    xl, core = lax.div(low, 2), lax.rem(low, 2)
    x = xh * 2 + xl
    chip = (y * 4 + x) * 8 + z
    partner = col + 1 - 2 * core
    half_r = lax.div(y, 2)
    half_z = lax.div(z, 4)

    barrier = pltpu.get_barrier_semaphore()

    def greet_row(t, _):
        pl.semaphore_signal(
            barrier, inc=1, device_id=(lax.rem(row + t, 8), col), device_id_type=MESH
        )
        return 0

    def greet_col(t, _):
        pl.semaphore_signal(
            barrier, inc=1, device_id=(row, lax.rem(col + t, 32)), device_id_type=MESH
        )
        return 0

    lax.fori_loop(1, 8, greet_row, 0)
    lax.fori_loop(1, 32, greet_col, 0)

    def prepare(u):
        w_t[u] = jnp.transpose(proj_w[u, :, 0:512].astype(F32)).astype(BF16)
        bias_t[u] = jnp.transpose(
            jnp.broadcast_to(proj_b[u : u + 1, 0:512], (128, 512))
        )
        mgain_t[u] = jnp.transpose(jnp.broadcast_to(mid_gain[u : u + 1, :], (128, 128)))
        mbias_t[u] = jnp.transpose(jnp.broadcast_to(mid_bias[u : u + 1, :], (128, 128)))

    def project(u, s, values):
        normed = norm_rows(values, in_gain[u : u + 1, :], in_bias[u : u + 1, :]).astype(BF16)

        def part(first):
            return (
                lax.dot_general(
                    w_t[u, first : first + 128, :],
                    normed,
                    (((1,), (1,)), ((), ())),
                    preferred_element_type=F32,
                )
                + bias_t[u, first : first + 128, :]
            )

        tmp_r[pl.ds(s, 128, stride=8), :] = jax.nn.sigmoid(part(384)) * part(256)
        tmp_l[pl.ds(s, 128, stride=8), :] = jax.nn.sigmoid(part(128)) * part(0)
        gates[s] = jax.nn.sigmoid(
            jnp.dot(normed, proj_w[u, :, 512:640], preferred_element_type=F32)
            + proj_b[u : u + 1, 512:640]
        )

    def pack(u):
        def some(n, _):
            rows = pl.ds(n * 128, 128)
            send_r[u, pl.ds(n * 16, 16)] = tmp_r[rows, :].reshape(16, 8, 128).astype(BF16)
            send_l[u, pl.ds(n * 16, 16)] = tmp_l[rows, :].reshape(16, 8, 128).astype(BF16)
            return 0

        lax.fori_loop(0, 8, some, 0)

    def target(t):
        tz = lax.rem(z + lax.rem(t, 8), 8)
        tx = lax.rem(x + lax.rem(lax.div(t, 8), 4), 4)
        ty = lax.rem(y + lax.div(t, 32), 4)
        there = (ty * 4 + tx) * 8 + tz
        return there, ty * 2 + lax.div(tx, 2), tz * 4 + lax.rem(tx, 2) * 2

    def bytes_wait(buffer, sem):
        pltpu.make_async_copy(buffer, buffer, sem).wait()

    def send_right(u):
        slot = (core * 8 + row) * 16 + lax.div(col, 2)

        def one(t, _):
            there, trow, tcol = target(t)
            pltpu.make_async_remote_copy(
                send_r.at[u, there], recv_r.at[u, slot], sems_send.at[u, 0], sems_recv.at[u, 0],
                device_id=(trow, tcol + core), device_id_type=MESH,
            ).start()
            return 0

        lax.fori_loop(1, 128, one, 0)
        recv_r[u, slot] = send_r[u, chip]

    def send_left(u, half):
        if u == 0:
            slot = (core * 4 + lax.rem(row, 4)) * 16 + lax.div(col, 2)
        else:
            slot = (core * 8 + row) * 8 + lax.rem(lax.div(col, 2), 8)

        def one(t, _):
            there, trow, tcol = target(t)
            pltpu.make_async_remote_copy(
                send_l.at[u, there], recv_l.at[u, slot], sems_send.at[u, 1], sems_recv.at[u, 1],
                device_id=(trow, tcol + half), device_id_type=MESH,
            ).start()
            return 0

        lax.fori_loop(1, 128, one, 0)

        @pl.when(core == half)
        def _():
            recv_l[u, slot] = send_l[u, chip]

        @pl.when(core != half)
        def _():
            one(0, 0)

    def send_mixed(u):
        def one(t, _):
            tz = lax.rem(z + lax.rem(t, 8), 8)
            rest = lax.div(t, 8)
            tlow = lax.rem(low + lax.rem(rest, 4), 4)
            trow = lax.rem(row + lax.div(rest, 4), 4)
            tcol = tz * 4 + tlow
            pltpu.make_async_remote_copy(
                send_m.at[u, trow * 32 + tcol], recv_m.at[u, chip],
                sems_send.at[u, 2], sems_recv.at[u, 2],
                device_id=(core * 4 + trow, tcol), device_id_type=MESH,
            ).start()
            return 0

        lax.fori_loop(1, 128, one, 0)

        @pl.when(core == half_r)
        def _():
            recv_m[u, chip] = send_m[u, lax.rem(row, 4) * 32 + col]

        @pl.when(core != half_r)
        def _():
            one(0, 0)

    def wait_messages(buffer, sem, short):
        @pl.when(short)
        def _():
            bytes_wait(buffer.at[pl.ds(0, 127)], sem)

        @pl.when(jnp.logical_not(short))
        def _():
            bytes_wait(buffer, sem)

    def share_right(u):
        bytes_wait(recv_r.at[u, pl.ds(0, 127)], sems_recv.at[u, 0])
        mine = pl.ds(core * 128, 128)
        copy = pltpu.make_async_remote_copy(
            recv_r.at[u, mine], recv_r.at[u, mine], sems_send.at[u, 3], sems_recv.at[u, 3],
            device_id=(row, partner), device_id_type=MESH,
        )
        copy.start()
        return copy

    def woven(first, second):
        first, second = first.astype(F32), second.astype(F32)
        lane = lax.broadcasted_iota(jnp.int32, first.shape, 2)
        low_half = jnp.where(lane < 64, first, pltpu.roll(second, 64, 2))
        high_half = jnp.where(lane < 64, pltpu.roll(first, 64, 2), second)
        return jnp.concatenate([low_half, high_half], axis=1).astype(BF16)

    def arrange_right(u):
        for par in range(2):
            for p in range(4):
                base = (par * 8 + 2 * p) * 16
                a_r[:, par, :, p * 128 : (p + 1) * 128] = woven(
                    recv_r[u, base : base + 16], recv_r[u, base + 16 : base + 32]
                )

    def arrange_left(u):
        for par in range(2):
            if u == 0:
                for p in range(2):
                    base = (par * 4 + 2 * p) * 16
                    a_l0[:, par, :, p * 128 : (p + 1) * 128] = woven(
                        recv_l[u, base : base + 16], recv_l[u, base + 16 : base + 32]
                    )
            else:
                for p in range(4):
                    base = (par * 8 + 2 * p) * 8
                    a_l1[:, par, :, p * 128 : (p + 1) * 128] = woven(
                        recv_l[u, base : base + 8], recv_l[u, base + 8 : base + 16]
                    )

    def contract(u):
        right = a_r[...].reshape(512, 512)
        if u == 0:
            left = a_l0[...].reshape(512, 256)
            mixed[...] = lax.dot_general(
                right, left, (((0,), (0,)), ((), ())), preferred_element_type=F32
            )
        else:
            left = a_l1[...].reshape(256, 512)
            mixed[...] = lax.dot_general(
                right, left, (((1,), (1,)), ((), ())), preferred_element_type=F32
            )

    def pack_mixed(u):
        for p in range(2):
            both = mixed[:, p * 128 : (p + 1) * 128].reshape(32, 2, 8, 128)
            low_rows, high_rows = both[:, 0], both[:, 1]
            lane = lax.broadcasted_iota(jnp.int32, low_rows.shape, 2)
            send_m[u, 64 * p : 64 * p + 32] = jnp.where(
                lane < 64, low_rows, pltpu.roll(high_rows, 64, 2)
            ).astype(BF16)
            send_m[u, 64 * p + 32 : 64 * p + 64] = jnp.where(
                lane < 64, pltpu.roll(low_rows, 64, 2), high_rows
            ).astype(BF16)

    def normalise_mixed(u):
        def total(n, acc):
            return acc + jnp.sum(recv_m[u, pl.ds(n * 16, 16)].astype(F32), axis=0)

        mean = lax.fori_loop(0, 8, total, jnp.zeros((8, 128), F32)) * (1.0 / 128)

        def spread(n, acc):
            centred = recv_m[u, pl.ds(n * 16, 16)].astype(F32) - mean[None]
            return acc + jnp.sum(centred * centred, axis=0)

        variance = lax.fori_loop(0, 8, spread, jnp.zeros((8, 128), F32)) * (1.0 / 128)
        scale = lax.rsqrt(variance + EPS)

        def put(n, _):
            centred = recv_m[u, pl.ds(n * 16, 16)].astype(F32) - mean[None]
            tmp_l[pl.ds(n * 128, 128), :] = (centred * scale[None]).reshape(128, 128)
            return 0

        lax.fori_loop(0, 8, put, 0)

    def finish(u, s):
        middle = (tmp_l[pl.ds(s, 128, stride=8), :] * mgain_t[u] + mbias_t[u]).astype(BF16)
        outcome = (
            lax.dot_general(
                middle, out_w[u], (((0,), (0,)), ((), ())), preferred_element_type=F32
            )
            + out_b[u : u + 1, :]
        )
        return state[s] + gates[s] * outcome

    def exchange(u, half, cover):
        pack(u)
        send_right(u)
        send_left(u, half)
        cover()
        shared = share_right(u)
        wait_messages(recv_l.at[u], sems_recv.at[u, 1], core == half)
        arrange_left(u)
        shared.wait_recv()
        arrange_right(u)
        contract(u)
        pack_mixed(u)
        send_mixed(u)
        wait_messages(recv_m.at[u], sems_recv.at[u, 2], core == half_r)
        normalise_mixed(u)
        return shared

    prepare(0)

    def first(s, _):
        values = jnp.concatenate(
            [pair_ref[pl.ds(s, 64, stride=16), :], pair_ref[pl.ds(s + 8, 64, stride=16), :]], axis=0
        )
        state[s] = values
        project(0, s, values)
        return 0

    lax.fori_loop(0, 8, first, 0)

    pl.semaphore_wait(barrier, 38)

    def greet_again(t, _):
        pl.semaphore_signal(
            sem_enter, inc=1, device_id=(lax.rem(row + t, 8), col), device_id_type=MESH
        )
        return 0

    lax.fori_loop(1, 8, greet_again, 0)
    pl.semaphore_wait(sem_enter, 7)

    shared0 = exchange(0, half_r, lambda: prepare(1))

    def middle_step(s, _):
        values = finish(0, s)
        state[s] = values
        project(1, s, values)
        return 0

    lax.fori_loop(0, 8, middle_step, 0)

    shared1 = exchange(1, half_z, lambda: None)

    def last(s, _):
        values = finish(1, s)
        out_ref[pl.ds(s, 64, stride=16), :] = values[0:64]
        out_ref[pl.ds(s + 8, 64, stride=16), :] = values[64:128]
        return 0

    lax.fori_loop(0, 8, last, 0)

    for u, shared, half in ((0, shared0, half_r), (1, shared1, half_z)):
        shared.wait_send()
        bytes_wait(send_r.at[u, pl.ds(0, 127)], sems_send.at[u, 0])
        wait_messages(send_l.at[u], sems_send.at[u, 1], core == half)
        wait_messages(send_m.at[u], sems_send.at[u, 2], core == half_r)


def body(pair, in_gain, in_bias, proj_weight, proj_bias, mid_gain, mid_bias, out_weight, out_bias):
    vmem = pl.BlockSpec(memory_space=pltpu.VMEM)
    out = pl.pallas_call(
        kernel,
        out_shape=jax.ShapeDtypeStruct((1024, 128), F32),
        in_specs=[vmem] * 9,
        out_specs=vmem,
        scratch_shapes=[
            pltpu.VMEM((2, 512, 128), BF16),
            pltpu.VMEM((2, 512, 128), F32),
            pltpu.VMEM((2, 128, 128), F32),
            pltpu.VMEM((2, 128, 128), F32),
            pltpu.VMEM((8, 128, 128), F32),
            pltpu.VMEM((8, 128, 128), F32),
            pltpu.VMEM((1024, 128), F32),
            pltpu.VMEM((1024, 128), F32),
            pltpu.VMEM((2, 128, 8, 128), BF16),
            pltpu.VMEM((2, 128, 8, 128), BF16),
            pltpu.VMEM((2, 128, 8, 128), BF16),
            pltpu.VMEM((2, 128, 8, 128), BF16),
            pltpu.VMEM((2, 256, 8, 128), BF16),
            pltpu.VMEM((2, 128, 8, 128), BF16),
            pltpu.VMEM((16, 2, 16, 256), BF16),
            pltpu.VMEM((8, 2, 16, 512), BF16),
            pltpu.VMEM((16, 2, 16, 512), BF16),
            pltpu.VMEM((512, 256), F32),
            pltpu.SemaphoreType.DMA((2, 4)),
            pltpu.SemaphoreType.DMA((2, 4)),
            pltpu.SemaphoreType.REGULAR,
        ],
        compiler_params=pltpu.CompilerParams(
            collective_id=0, has_side_effects=True, vmem_limit_bytes=32 * 1024 * 1024
        ),
    )(
        pair.reshape(1024, 128), in_gain, in_bias, proj_weight, proj_bias,
        mid_gain, mid_bias, out_weight, out_bias,
    )
    return out.reshape(64, 16, 128)


def solution(mesh):
    placed = (P("row", "col", None), P(), P(), P(), P(), P(), P(), P(), P())
    return jax.shard_map(
        body, mesh=mesh, in_specs=placed, out_specs=P("row", "col", None), check_vma=False
    )
```

time: 365 us -> 87.1 us (0.24)
  waiting for transfers between devices: 151 us -> 0 us
  blocking collectives: 81.7 us -> 0 us
  Pallas kernels: 0 us -> 79 us
  local copies, waits for them, and re-layouts: 74.6 us -> 7.73 us
  matrix products: 21.1 us -> 0 us
  starting transfers between devices: 14.9 us -> 0 us
  between operations: 13.6 us -> 0.02 us
  other arithmetic: 6.47 us -> 0 us
    all_gather x2 -> x0, waiting for transfers between devices: 86.6 us -> none  [body(): lax.all_gather(left, 'col', axis=2, tiled=True)]
    all_to_all x2 -> x0, blocking collectives: 81.7 us -> none  [the longest x1 48.4 us: copy_for_each(): lax.all_to_all(jnp.broadcast_to(value[None], (peers, *value.shape)), axis...]
    pallas_call x0 -> x1, Pallas kernels: none -> 79 us  [body(): pl.pallas_call(kernel, out_shape=jax.ShapeDtypeStruct((1024, 128), F32),...]
    all_to_all x1 -> x0, waiting for transfers between devices: 64.4 us -> none  [body(): lax.all_to_all(strip, 'col', split_axis=1, concat_axis=2, tiled=True)]
    all_gather x2 -> x0, local copies, waits for them, and re-layouts: 58.3 us -> none  [body(): lax.all_gather(left, 'col', axis=2, tiled=True)]
    dot_general x6 -> x0, matrix products: 21.1 us -> none  [the longest x1 8.04 us: body(): jnp.einsum('cki,ckj->cij', lax.all_gather(left, 'col', axis=2, tiled=True...]
    all_to_all x1 -> x0, starting transfers between devices: 14.7 us -> none  [body(): lax.all_to_all(strip, 'col', split_axis=1, concat_axis=2, tiled=True)]
    all_to_all x2 -> x0, local copies, waits for them, and re-layouts: 5.32 us -> none  [body(): lax.all_to_all(strip, 'col', split_axis=1, concat_axis=2, tiled=True)]
  transfers between devices with their start and end apart: 3 -> 0, of which waited for: 2 -> 0; matrix products, arithmetic and copies ran while one was open for 2% -> 0% of each run, Pallas kernels for 0% -> 0%
where the time goes in v1:
time: 87.1 us; the launch traced here: 86.8 us
  Pallas kernels  79 us (91%)
  local copies, waits for them, and re-layouts  7.73 us (9%)
    pallas_call x1, Pallas kernels, body(): pl.pallas_call(kernel, out_shape=jax.ShapeDtypeStruct((1024, 128), F32),...  79 us
    unnamed x19, local copies, waits for them, and re-layouts  7.73 us

profile of v1, /device:TPU:1, one launch (start us, length us, event | category | flops | bytes accessed | tf_op | source)
XLA Modules:
  0.0 86.8 jit_solution(8652176285348349699)
XLA Ops:
  0.0 0.0 copy-start.4
  0.0 0.7 copy-done.4
  0.7 0.0 copy-start
  0.7 1.0 %copy-done = f32[64,16,128]{2,1,0:T(8,128)S(1)} copy-done((f32[64,16,128]{2,1,0:T(8,128)S(1)}, f32[64,16,128]{2,1,0:T(8,128)}, u32[]{:S(2)}) %copy-start) | copy-done | bytes 524312
  1.7 0.0 copy-start.1
  1.7 1.0 %copy-done.1 = bf16[2,128,640]{2,1,0:T(8,128)(2,1)S(1)} copy-done((bf16[2,128,640]{2,1,0:T(8,128)(2,1)S(1)}, bf16[2,128,640]{2,1,0:T(8,128)(2,1)}, u32[]{:S(2)}) %copy-start.1) | copy-done | bytes 327704
  2.7 0.0 copy-start.2
  2.7 0.8 copy-done.2
  3.5 0.0 copy-start.3
  3.5 0.7 copy-done.3
  4.2 0.0 copy-start.5
  4.2 0.7 copy-done.5
  4.9 0.0 copy-start.6
  4.9 0.7 copy-done.6
  5.6 0.0 copy-start.7
  5.6 0.7 copy-done.7
  6.3 0.0 copy-start.8
  6.3 0.7 copy-done.8
  6.9 79.0 %shard_map.91 = f32[1024,128]{1,0:T(8,128)S(1)} custom-call(f32[1024,128]{1,0:T(8,128)S(1)} %bitcast.3, f32[2,128]{1,0:T(2,128)S(1)} %copy-done.4, f32[2,128]{1,0:T(2,128)S(1)} %copy-done.5, bf16[2,128,640]{2,1,0:T(8,128)(2,1)S(1)} %copy-done.1, f32[2,640]{1,0:T(2,128)S(1)} %copy-done.3, f32[2,128]{1,0:T(2,128)S(1)} %copy-done.6, f32[2,128]{1,0:T(2,128)S(1)} %copy-done.7, ...), custom_call_target="tpu_custom_call" | custom-call | tf_op jit(solution)/shard_map/pallas_call | solution.py:343
  86.0 0.8 copy.11
Async XLA Ops:
  0.0 0.7 copy-start.4
  0.7 1.0 %copy-start = (f32[64,16,128]{2,1,0:T(8,128)S(1)}, f32[64,16,128]{2,1,0:T(8,128)}, u32[]{:S(2)}) copy-start(f32[64,16,128]{2,1,0:T(8,128)} %param.9) | copy-start | bytes 1572868
  1.7 1.0 %copy-start.1 = (bf16[2,128,640]{2,1,0:T(8,128)(2,1)S(1)}, bf16[2,128,640]{2,1,0:T(8,128)(2,1)}, u32[]{:S(2)}) copy-start(bf16[2,128,640]{2,1,0:T(8,128)(2,1)} %proj_w.1) | copy-start | bytes 983044
  2.7 0.8 copy-start.2
  3.5 0.7 copy-start.3
  4.2 0.7 copy-start.5
  4.9 0.7 copy-start.6
  5.6 0.7 copy-start.7
  6.3 0.7 copy-start.8

commit v2 on v1

--- a/solution.py
+++ b/solution.py
@@ -11,6 +11,7 @@
 F32 = jnp.float32
 BF16 = jnp.bfloat16
 EPS = 1e-05
+FAR, SPLIT, CORE_FIRST = True, True, True
 
 
 def norm_rows(values, gain, offset):
@@ -21,8 +22,10 @@
 
 
 def kernel(
-    pair_ref, in_gain, in_bias, proj_w, proj_b, mid_gain, mid_bias, out_w, out_b,
+    pair_in, in_gain_in, in_bias_in, proj_w_in, proj_b_in, mid_gain_in, mid_bias_in,
+    out_w_in, out_b_in,
     out_ref,
+    pair_ref, in_gain, in_bias, proj_w, proj_b, mid_gain, mid_bias, out_w, out_b, sems_in,
     w_t, bias_t, mgain_t, mbias_t,
     state, gates, tmp_l, tmp_r,
     send_l, send_r, send_m, recv_l, recv_r, recv_m,
@@ -57,6 +60,19 @@
     lax.fori_loop(1, 8, greet_row, 0)
     lax.fori_loop(1, 32, greet_col, 0)
 
+    loads = [
+        pltpu.make_async_copy(source, held, sems_in.at[n])
+        for n, (source, held) in enumerate(
+            (
+                (proj_w_in, proj_w), (proj_b_in, proj_b), (mid_gain_in, mid_gain),
+                (mid_bias_in, mid_bias), (in_gain_in, in_gain), (in_bias_in, in_bias),
+                (pair_in, pair_ref), (out_w_in, out_w), (out_b_in, out_b),
+            )
+        )
+    ]
+    for load in loads:
+        load.start()
+
     def prepare(u):
         w_t[u] = jnp.transpose(proj_w[u, :, 0:512].astype(F32)).astype(BF16)
         bias_t[u] = jnp.transpose(
@@ -95,77 +111,114 @@
 
         lax.fori_loop(0, 8, some, 0)
 
-    def target(t):
-        tz = lax.rem(z + lax.rem(t, 8), 8)
-        tx = lax.rem(x + lax.rem(lax.div(t, 8), 4), 4)
-        ty = lax.rem(y + lax.div(t, 32), 4)
+    def place(tx, ty, tz):
         there = (ty * 4 + tx) * 8 + tz
         return there, ty * 2 + lax.div(tx, 2), tz * 4 + lax.rem(tx, 2) * 2
 
+    def far(n, size):
+        return lax.select(
+            lax.rem(n, 2) == 1, size // 2 - lax.div(n + 1, 2), size // 2 + lax.div(n, 2)
+        )
+
+    def target(t):
+        dz, dx, dy = lax.rem(t, 8), lax.rem(lax.div(t, 8), 4), lax.rem(lax.div(t, 32), 4)
+        if FAR:
+            dz, dx, dy = far(dz, 8), far(dx, 4), far(dy, 4)
+        if not SPLIT:
+            return place(lax.rem(x + dx, 4), lax.rem(y + dy, 4), lax.rem(z + dz, 8))
+        part, rest = lax.div(t, 64), lax.rem(t, 64)
+        dz, dx, dy = lax.rem(rest, 8), lax.rem(lax.div(rest, 8), 4), lax.div(rest, 32)
+        if FAR:
+            dz, dx, dy = far(dz, 8), far(dx, 4), 1 - dy
+        tz, tx = lax.rem(z + dz, 8), lax.rem(x + dx, 4)
+        ty = 2 * lax.rem(lax.div(y, 2) + dy, 2) + lax.rem(part + tx + tz, 2)
+        return place(tx, ty, tz)
+
     def bytes_wait(buffer, sem):
         pltpu.make_async_copy(buffer, buffer, sem).wait()
 
-    def send_right(u):
-        slot = (core * 8 + row) * 16 + lax.div(col, 2)
-
-        def one(t, _):
+    def exchange_sends(u, half):
+        slot_r = (core * 8 + row) * 16 + lax.div(col, 2)
+        if u == 0:
+            slot_l = (core * 4 + lax.rem(row, 4)) * 16 + lax.div(col, 2)
+        else:
+            slot_l = (core * 8 + row) * 8 + lax.rem(lax.div(col, 2), 8)
+
+        def right(t, _):
             there, trow, tcol = target(t)
-            pltpu.make_async_remote_copy(
-                send_r.at[u, there], recv_r.at[u, slot], sems_send.at[u, 0], sems_recv.at[u, 0],
-                device_id=(trow, tcol + core), device_id_type=MESH,
-            ).start()
+
+            @pl.when(there != chip)
+            def _():
+                pltpu.make_async_remote_copy(
+                    send_r.at[u, there], recv_r.at[u, slot_r],
+                    sems_send.at[u, 0], sems_recv.at[u, 0],
+                    device_id=(trow, tcol + core), device_id_type=MESH,
+                ).start()
+
             return 0
 
-        lax.fori_loop(1, 128, one, 0)
-        recv_r[u, slot] = send_r[u, chip]
-
-    def send_left(u, half):
-        if u == 0:
-            slot = (core * 4 + lax.rem(row, 4)) * 16 + lax.div(col, 2)
+        def left(t, _):
+            there, trow, tcol = target(t)
+
+            @pl.when(jnp.logical_or(there != chip, core != half))
+            def _():
+                pltpu.make_async_remote_copy(
+                    send_l.at[u, there], recv_l.at[u, slot_l],
+                    sems_send.at[u, 1], sems_recv.at[u, 1],
+                    device_id=(trow, tcol + half), device_id_type=MESH,
+                ).start()
+
+            return 0
+
+        if SPLIT:
+            for part in range(2):
+                lax.fori_loop(64 * part, 64 * part + 64, right, 0)
+                lax.fori_loop(64 * part, 64 * part + 64, left, 0)
         else:
-            slot = (core * 8 + row) * 8 + lax.rem(lax.div(col, 2), 8)
-
-        def one(t, _):
-            there, trow, tcol = target(t)
-            pltpu.make_async_remote_copy(
-                send_l.at[u, there], recv_l.at[u, slot], sems_send.at[u, 1], sems_recv.at[u, 1],
-                device_id=(trow, tcol + half), device_id_type=MESH,
-            ).start()
-            return 0
-
-        lax.fori_loop(1, 128, one, 0)
+            lax.fori_loop(0, 128, right, 0)
+            lax.fori_loop(0, 128, left, 0)
+        recv_r[u, slot_r] = send_r[u, chip]
 
         @pl.when(core == half)
         def _():
-            recv_l[u, slot] = send_l[u, chip]
-
-        @pl.when(core != half)
-        def _():
-            one(0, 0)
+            recv_l[u, slot_l] = send_l[u, chip]
 
     def send_mixed(u):
         def one(t, _):
-            tz = lax.rem(z + lax.rem(t, 8), 8)
+            tz = lax.rem(t, 8)
             rest = lax.div(t, 8)
-            tlow = lax.rem(low + lax.rem(rest, 4), 4)
-            trow = lax.rem(row + lax.div(rest, 4), 4)
+            if FAR:
+                tz = far(tz, 8)
+            tz = lax.rem(z + tz, 8)
+            if CORE_FIRST and u == 0:
+                tcore, rest = lax.div(rest, 8), lax.rem(rest, 8)
+                if FAR:
+                    rest = 7 - rest
+                txl, rest = lax.rem(xl + rest, 2), lax.div(rest, 2)
+                tlow = txl * 2 + tcore
+            else:
+                if FAR:
+                    rest = 15 - rest
+                tlow = lax.rem(low + lax.rem(rest, 4), 4)
+                rest = lax.div(rest, 4)
+            trow = lax.rem(row + rest, 4)
             tcol = tz * 4 + tlow
-            pltpu.make_async_remote_copy(
-                send_m.at[u, trow * 32 + tcol], recv_m.at[u, chip],
-                sems_send.at[u, 2], sems_recv.at[u, 2],
-                device_id=(core * 4 + trow, tcol), device_id_type=MESH,
-            ).start()
+
+            @pl.when(jnp.logical_or(core * 4 + trow != row, tcol != col))
+            def _():
+                pltpu.make_async_remote_copy(
+                    send_m.at[u, trow * 32 + tcol], recv_m.at[u, chip],
+                    sems_send.at[u, 2], sems_recv.at[u, 2],
+                    device_id=(core * 4 + trow, tcol), device_id_type=MESH,
+                ).start()
+
             return 0
 
-        lax.fori_loop(1, 128, one, 0)
+        lax.fori_loop(0, 128, one, 0)
 
         @pl.when(core == half_r)
         def _():
             recv_m[u, chip] = send_m[u, lax.rem(row, 4) * 32 + col]
-
-        @pl.when(core != half_r)
-        def _():
-            one(0, 0)
 
     def wait_messages(buffer, sem, short):
         @pl.when(short)
@@ -273,14 +326,13 @@
 
     def exchange(u, half, cover):
         pack(u)
-        send_right(u)
-        send_left(u, half)
+        exchange_sends(u, half)
         cover()
         shared = share_right(u)
+        shared.wait_recv()
+        arrange_right(u)
         wait_messages(recv_l.at[u], sems_recv.at[u, 1], core == half)
         arrange_left(u)
-        shared.wait_recv()
-        arrange_right(u)
         contract(u)
         pack_mixed(u)
         send_mixed(u)
@@ -288,6 +340,8 @@
         normalise_mixed(u)
         return shared
 
+    for load in loads:
+        load.wait()
     prepare(0)
 
     def first(s, _):
@@ -343,9 +397,19 @@
     out = pl.pallas_call(
         kernel,
         out_shape=jax.ShapeDtypeStruct((1024, 128), F32),
-        in_specs=[vmem] * 9,
+        in_specs=[pl.BlockSpec(memory_space=pltpu.HBM)] * 9,
         out_specs=vmem,
         scratch_shapes=[
+            pltpu.VMEM((1024, 128), F32),
+            pltpu.VMEM((2, 128), F32),
+            pltpu.VMEM((2, 128), F32),
+            pltpu.VMEM((2, 128, 640), BF16),
+            pltpu.VMEM((2, 640), F32),
+            pltpu.VMEM((2, 128), F32),
+            pltpu.VMEM((2, 128), F32),
+            pltpu.VMEM((2, 128, 128), BF16),
+            pltpu.VMEM((2, 128), F32),
+            pltpu.SemaphoreType.DMA((9,)),
             pltpu.VMEM((2, 512, 128), BF16),
             pltpu.VMEM((2, 512, 128), F32),
             pltpu.VMEM((2, 128, 128), F32),
@@ -369,7 +433,7 @@
             pltpu.SemaphoreType.REGULAR,
         ],
         compiler_params=pltpu.CompilerParams(
-            collective_id=0, has_side_effects=True, vmem_limit_bytes=32 * 1024 * 1024
+            collective_id=0, has_side_effects=True
         ),
     )(
         pair.reshape(1024, 128), in_gain, in_bias, proj_weight, proj_bias,

time: 87.1 us -> 77.3 us (0.89)
  local copies, waits for them, and re-layouts: 7.73 us -> 1.87 us
  Pallas kernels: 79 us -> 75.3 us
    unnamed x19 -> x1, local copies, waits for them, and re-layouts: 7.73 us -> 1.87 us
    pallas_call x1, Pallas kernels: 79 us -> 75.3 us  [body(): pl.pallas_call(kernel, out_shape=jax.ShapeDtypeStruct((1024, 128), F32),...]
where the time goes in v2:
time: 77.3 us; the launch traced here: 77.2 us
  Pallas kernels  75.3 us (97%)
  local copies, waits for them, and re-layouts  1.87 us (2%)
    pallas_call x1, Pallas kernels, body(): pl.pallas_call(kernel, out_shape=jax.ShapeDtypeStruct((1024, 128), F32),...  75.3 us
    unnamed x1, local copies, waits for them, and re-layouts  1.87 us

profile of v2, /device:TPU:1, one launch (start us, length us, event | category | flops | bytes accessed | tf_op | source)
XLA Modules:
  0.0 77.2 jit_solution(14246991012034461936)
XLA Ops:
  0.0 75.3 %shard_map.91 = f32[1024,128]{1,0:T(8,128)} custom-call(f32[1024,128]{1,0:T(8,128)} %bitcast.3, f32[2,128]{1,0:T(2,128)} %in_gain_in.1, f32[2,128]{1,0:T(2,128)} %in_bias_in.1, bf16[2,128,640]{2,1,0:T(8,128)(2,1)} %proj_w_in.1, f32[2,640]{1,0:T(2,128)} %proj_b_in.1, f32[2,128]{1,0:T(2,128)} %mid_gain_in.1, f32[2,128]{1,0:T(2,128)} %mid_bias_in.1, ...), custom_call_target="tpu_custom_call" | custom-call | tf_op jit(solution)/shard_map/pallas_call | solution.py:397
  75.3 1.9 %copy.11 = f32[64,16,128]{2,1,0:T(8,128)} copy(f32[64,16,128]{2,1,0:T(8,128)} %bitcast.2) | data formatting | bytes 1048576

commit v3 on v2

--- a/solution.py
+++ b/solution.py
@@ -14,11 +14,15 @@
 FAR, SPLIT, CORE_FIRST = True, True, True
 
 
-def norm_rows(values, gain, offset):
-    mean = jnp.mean(values, -1, keepdims=True)
+def twice(column):
+    return jnp.concatenate([column, column], axis=1)
+
+
+def norm_channels(values, gain, offset):
+    mean = jnp.mean(values, 0, keepdims=True)
     centred = values - mean
-    variance = jnp.mean(centred * centred, -1, keepdims=True)
-    return centred * lax.rsqrt(variance + EPS) * gain + offset
+    variance = jnp.mean(centred * centred, 0, keepdims=True)
+    return (centred * lax.rsqrt(variance + EPS) * twice(gain) + twice(offset)).astype(BF16)
 
 
 def kernel(
@@ -26,8 +30,8 @@
     out_w_in, out_b_in,
     out_ref,
     pair_ref, in_gain, in_bias, proj_w, proj_b, mid_gain, mid_bias, out_w, out_b, sems_in,
-    w_t, bias_t, mgain_t, mbias_t,
-    state, gates, tmp_l, tmp_r,
+    w_t, ow_t, bias_t, igain_t, ibias_t, mgain_t, mbias_t, obias_t,
+    state, gates, tmp_l, tmp_r, tmp_m,
     send_l, send_r, send_m, recv_l, recv_r, recv_m,
     a_l0, a_l1, a_r, mixed,
     sems_send, sems_recv, sem_enter,
@@ -73,34 +77,36 @@
     for load in loads:
         load.start()
 
-    def prepare(u):
-        w_t[u] = jnp.transpose(proj_w[u, :, 0:512].astype(F32)).astype(BF16)
-        bias_t[u] = jnp.transpose(
-            jnp.broadcast_to(proj_b[u : u + 1, 0:512], (128, 512))
-        )
-        mgain_t[u] = jnp.transpose(jnp.broadcast_to(mid_gain[u : u + 1, :], (128, 128)))
-        mbias_t[u] = jnp.transpose(jnp.broadcast_to(mid_bias[u : u + 1, :], (128, 128)))
-
-    def project(u, s, values):
-        normed = norm_rows(values, in_gain[u : u + 1, :], in_bias[u : u + 1, :]).astype(BF16)
+    def column(held, u):
+        return jnp.transpose(jnp.broadcast_to(held[u : u + 1, :], (128, held.shape[1])))
+
+    def prepare_projection(u):
+        w_t[u] = jnp.transpose(proj_w[u].astype(F32)).astype(BF16)
+        igain_t[u] = column(in_gain, u)
+        ibias_t[u] = column(in_bias, u)
+        bias_t[u] = column(proj_b, u)
+
+    def prepare_finish(u):
+        ow_t[u] = jnp.transpose(out_w[u].astype(F32)).astype(BF16)
+        mgain_t[u] = column(mid_gain, u)
+        mbias_t[u] = column(mid_bias, u)
+        obias_t[u] = column(out_b, u)
+
+    def project(u, n, values):
+        normed = norm_channels(values, igain_t[u], ibias_t[u])
 
         def part(first):
-            return (
-                lax.dot_general(
-                    w_t[u, first : first + 128, :],
-                    normed,
-                    (((1,), (1,)), ((), ())),
-                    preferred_element_type=F32,
-                )
-                + bias_t[u, first : first + 128, :]
-            )
-
-        tmp_r[pl.ds(s, 128, stride=8), :] = jax.nn.sigmoid(part(384)) * part(256)
-        tmp_l[pl.ds(s, 128, stride=8), :] = jax.nn.sigmoid(part(128)) * part(0)
-        gates[s] = jax.nn.sigmoid(
-            jnp.dot(normed, proj_w[u, :, 512:640], preferred_element_type=F32)
-            + proj_b[u : u + 1, 512:640]
-        )
+            return jnp.dot(
+                w_t[u, first : first + 128, :], normed, preferred_element_type=F32
+            ) + twice(bias_t[u, first : first + 128, :])
+
+        right = jax.nn.sigmoid(part(384)) * part(256)
+        left = jax.nn.sigmoid(part(128)) * part(0)
+        for k in range(2):
+            rows = pl.ds(2 * n + k, 128, stride=8)
+            tmp_r[rows, :] = right[:, 128 * k : 128 * k + 128]
+            tmp_l[rows, :] = left[:, 128 * k : 128 * k + 128]
+        gates[n] = jax.nn.sigmoid(part(512))
 
     def pack(u):
         def some(n, _):
@@ -294,35 +300,22 @@
                 lane < 64, pltpu.roll(low_rows, 64, 2), high_rows
             ).astype(BF16)
 
-    def normalise_mixed(u):
-        def total(n, acc):
-            return acc + jnp.sum(recv_m[u, pl.ds(n * 16, 16)].astype(F32), axis=0)
-
-        mean = lax.fori_loop(0, 8, total, jnp.zeros((8, 128), F32)) * (1.0 / 128)
-
-        def spread(n, acc):
-            centred = recv_m[u, pl.ds(n * 16, 16)].astype(F32) - mean[None]
-            return acc + jnp.sum(centred * centred, axis=0)
-
-        variance = lax.fori_loop(0, 8, spread, jnp.zeros((8, 128), F32)) * (1.0 / 128)
-        scale = lax.rsqrt(variance + EPS)
-
+    def widen_mixed(u):
         def put(n, _):
-            centred = recv_m[u, pl.ds(n * 16, 16)].astype(F32) - mean[None]
-            tmp_l[pl.ds(n * 128, 128), :] = (centred * scale[None]).reshape(128, 128)
+            tmp_m[pl.ds(n * 128, 128), :] = (
+                recv_m[u, pl.ds(n * 16, 16)].astype(F32).reshape(128, 128)
+            )
             return 0
 
-        lax.fori_loop(0, 8, put, 0)
-
-    def finish(u, s):
-        middle = (tmp_l[pl.ds(s, 128, stride=8), :] * mgain_t[u] + mbias_t[u]).astype(BF16)
-        outcome = (
-            lax.dot_general(
-                middle, out_w[u], (((0,), (0,)), ((), ())), preferred_element_type=F32
-            )
-            + out_b[u : u + 1, :]
-        )
-        return state[s] + gates[s] * outcome
+        lax.fori_loop(0, 8, put, 0, unroll=True)
+
+    def finish(u, n):
+        values = jnp.concatenate(
+            [tmp_m[pl.ds(2 * n + k, 128, stride=8), :] for k in range(2)], axis=1
+        )
+        middle = norm_channels(values, mgain_t[u], mbias_t[u])
+        outcome = jnp.dot(ow_t[u], middle, preferred_element_type=F32) + twice(obias_t[u])
+        return state[n] + gates[n] * outcome
 
     def exchange(u, half, cover):
         pack(u)
@@ -337,22 +330,24 @@
         pack_mixed(u)
         send_mixed(u)
         wait_messages(recv_m.at[u], sems_recv.at[u, 2], core == half_r)
-        normalise_mixed(u)
+        widen_mixed(u)
         return shared
 
     for load in loads:
         load.wait()
-    prepare(0)
-
-    def first(s, _):
-        values = jnp.concatenate(
-            [pair_ref[pl.ds(s, 64, stride=16), :], pair_ref[pl.ds(s + 8, 64, stride=16), :]], axis=0
-        )
-        state[s] = values
-        project(0, s, values)
-        return 0
-
-    lax.fori_loop(0, 8, first, 0)
+    prepare_projection(0)
+
+    for n in range(4):
+        blocks = [
+            jnp.concatenate(
+                [pair_ref[pl.ds(s, 64, stride=16), :], pair_ref[pl.ds(s + 8, 64, stride=16), :]],
+                axis=0,
+            )
+            for s in (2 * n, 2 * n + 1)
+        ]
+        values = jnp.concatenate([jnp.transpose(block) for block in blocks], axis=1)
+        state[n] = values
+        project(0, n, values)
 
     pl.semaphore_wait(barrier, 38)
 
@@ -365,25 +360,27 @@
     lax.fori_loop(1, 8, greet_again, 0)
     pl.semaphore_wait(sem_enter, 7)
 
-    shared0 = exchange(0, half_r, lambda: prepare(1))
-
-    def middle_step(s, _):
-        values = finish(0, s)
-        state[s] = values
-        project(1, s, values)
-        return 0
-
-    lax.fori_loop(0, 8, middle_step, 0)
+    def cover():
+        prepare_finish(0)
+        prepare_projection(1)
+        prepare_finish(1)
+
+    shared0 = exchange(0, half_r, cover)
+
+    for n in range(4):
+        values = finish(0, n)
+        state[n] = values
+        project(1, n, values)
 
     shared1 = exchange(1, half_z, lambda: None)
 
-    def last(s, _):
-        values = finish(1, s)
-        out_ref[pl.ds(s, 64, stride=16), :] = values[0:64]
-        out_ref[pl.ds(s + 8, 64, stride=16), :] = values[64:128]
-        return 0
-
-    lax.fori_loop(0, 8, last, 0)
+    for n in range(4):
+        values = finish(1, n)
+        for k in range(2):
+            s = 2 * n + k
+            block = jnp.transpose(values[:, 128 * k : 128 * k + 128])
+            out_ref[pl.ds(s, 64, stride=16), :] = block[0:64]
+            out_ref[pl.ds(s + 8, 64, stride=16), :] = block[64:128]
 
     for u, shared, half in ((0, shared0, half_r), (1, shared1, half_z)):
         shared.wait_send()
@@ -410,12 +407,17 @@
             pltpu.VMEM((2, 128, 128), BF16),
             pltpu.VMEM((2, 128), F32),
             pltpu.SemaphoreType.DMA((9,)),
-            pltpu.VMEM((2, 512, 128), BF16),
-            pltpu.VMEM((2, 512, 128), F32),
+            pltpu.VMEM((2, 640, 128), BF16),
+            pltpu.VMEM((2, 128, 128), BF16),
+            pltpu.VMEM((2, 640, 128), F32),
             pltpu.VMEM((2, 128, 128), F32),
             pltpu.VMEM((2, 128, 128), F32),
-            pltpu.VMEM((8, 128, 128), F32),
-            pltpu.VMEM((8, 128, 128), F32),
+            pltpu.VMEM((2, 128, 128), F32),
+            pltpu.VMEM((2, 128, 128), F32),
+            pltpu.VMEM((2, 128, 128), F32),
+            pltpu.VMEM((4, 128, 256), F32),
+            pltpu.VMEM((4, 128, 256), F32),
+            pltpu.VMEM((1024, 128), F32),
             pltpu.VMEM((1024, 128), F32),
             pltpu.VMEM((1024, 128), F32),
             pltpu.VMEM((2, 128, 8, 128), BF16),

time: 77.3 us -> 71.7 us (0.928)
  Pallas kernels: 75.3 us -> 69.7 us
    pallas_call x1, Pallas kernels: 75.3 us -> 69.7 us  [body(): pl.pallas_call(kernel, out_shape=jax.ShapeDtypeStruct((1024, 128), F32),...]
where the time goes in v3:
time: 71.7 us; the launch traced here: 71.6 us
  Pallas kernels  69.7 us (97%)
  local copies, waits for them, and re-layouts  1.87 us (3%)
    pallas_call x1, Pallas kernels, body(): pl.pallas_call(kernel, out_shape=jax.ShapeDtypeStruct((1024, 128), F32),...  69.7 us
    unnamed x1, local copies, waits for them, and re-layouts  1.87 us

profile of v3, /device:TPU:1, one launch (start us, length us, event | category | flops | bytes accessed | tf_op | source)
XLA Modules:
  0.0 71.6 jit_solution(16420132314861117268)
XLA Ops:
  0.0 69.7 %shard_map.91 = f32[1024,128]{1,0:T(8,128)} custom-call(f32[1024,128]{1,0:T(8,128)} %bitcast.3, f32[2,128]{1,0:T(2,128)} %in_gain_in.1, f32[2,128]{1,0:T(2,128)} %in_bias_in.1, bf16[2,128,640]{2,1,0:T(8,128)(2,1)} %proj_w_in.1, f32[2,640]{1,0:T(2,128)} %proj_b_in.1, f32[2,128]{1,0:T(2,128)} %mid_gain_in.1, f32[2,128]{1,0:T(2,128)} %mid_bias_in.1, ...), custom_call_target="tpu_custom_call" | custom-call | tf_op jit(solution)/shard_map/pallas_call | solution.py:394
  69.7 1.9 %copy.11 = f32[64,16,128]{2,1,0:T(8,128)} copy(f32[64,16,128]{2,1,0:T(8,128)} %bitcast.2) | data formatting | bytes 1048576

commit v4 on v3

--- a/solution.py
+++ b/solution.py
@@ -11,7 +11,7 @@
 F32 = jnp.float32
 BF16 = jnp.bfloat16
 EPS = 1e-05
-FAR, SPLIT, CORE_FIRST = True, True, True
+UNROLL = 8
 
 
 def twice(column):
@@ -33,7 +33,7 @@
     w_t, ow_t, bias_t, igain_t, ibias_t, mgain_t, mbias_t, obias_t,
     state, gates, tmp_l, tmp_r, tmp_m,
     send_l, send_r, send_m, recv_l, recv_r, recv_m,
-    a_l0, a_l1, a_r, mixed,
+    a_l0, a_l1, a_r, a_rt, normed,
     sems_send, sems_recv, sem_enter,
 ):
     row = lax.axis_index("row")
@@ -92,30 +92,27 @@
         mbias_t[u] = column(mid_bias, u)
         obias_t[u] = column(out_b, u)
 
-    def project(u, n, values):
-        normed = norm_channels(values, igain_t[u], ibias_t[u])
-
-        def part(first):
-            return jnp.dot(
-                w_t[u, first : first + 128, :], normed, preferred_element_type=F32
-            ) + twice(bias_t[u, first : first + 128, :])
-
-        right = jax.nn.sigmoid(part(384)) * part(256)
-        left = jax.nn.sigmoid(part(128)) * part(0)
-        for k in range(2):
-            rows = pl.ds(2 * n + k, 128, stride=8)
-            tmp_r[rows, :] = right[:, 128 * k : 128 * k + 128]
-            tmp_l[rows, :] = left[:, 128 * k : 128 * k + 128]
-        gates[n] = jax.nn.sigmoid(part(512))
-
-    def pack(u):
-        def some(n, _):
-            rows = pl.ds(n * 128, 128)
-            send_r[u, pl.ds(n * 16, 16)] = tmp_r[rows, :].reshape(16, 8, 128).astype(BF16)
-            send_l[u, pl.ds(n * 16, 16)] = tmp_l[rows, :].reshape(16, 8, 128).astype(BF16)
-            return 0
-
-        lax.fori_loop(0, 8, some, 0)
+    def normalise(u, n, values):
+        normed[n] = norm_channels(values, igain_t[u], ibias_t[u])
+
+    def part(u, n, first):
+        return jnp.dot(
+            w_t[u, first : first + 128, :], normed[n], preferred_element_type=F32
+        ) + twice(bias_t[u, first : first + 128, :])
+
+    def project(u, first, held, packed):
+        for n in range(4):
+            values = jax.nn.sigmoid(part(u, n, first + 128)) * part(u, n, first)
+            for k in range(2):
+                held[pl.ds(2 * n + k, 128, stride=8), :] = values[:, 128 * k : 128 * k + 128]
+        for n in range(8):
+            packed[u, 16 * n : 16 * n + 16] = (
+                held[128 * n : 128 * n + 128, :].reshape(16, 8, 128).astype(BF16)
+            )
+
+    def open_gates(u):
+        for n in range(4):
+            gates[n] = jax.nn.sigmoid(part(u, n, 512))
 
     def place(tx, ty, tz):
         there = (ty * 4 + tx) * 8 + tz
@@ -127,87 +124,73 @@
         )
 
     def target(t):
-        dz, dx, dy = lax.rem(t, 8), lax.rem(lax.div(t, 8), 4), lax.rem(lax.div(t, 32), 4)
-        if FAR:
-            dz, dx, dy = far(dz, 8), far(dx, 4), far(dy, 4)
-        if not SPLIT:
-            return place(lax.rem(x + dx, 4), lax.rem(y + dy, 4), lax.rem(z + dz, 8))
         part, rest = lax.div(t, 64), lax.rem(t, 64)
-        dz, dx, dy = lax.rem(rest, 8), lax.rem(lax.div(rest, 8), 4), lax.div(rest, 32)
-        if FAR:
-            dz, dx, dy = far(dz, 8), far(dx, 4), 1 - dy
-        tz, tx = lax.rem(z + dz, 8), lax.rem(x + dx, 4)
-        ty = 2 * lax.rem(lax.div(y, 2) + dy, 2) + lax.rem(part + tx + tz, 2)
+        tz = lax.rem(z + far(lax.rem(rest, 8), 8), 8)
+        tx = lax.rem(x + far(lax.rem(lax.div(rest, 8), 4), 4), 4)
+        ty = 2 * lax.rem(lax.div(y, 2) + 1 - lax.div(rest, 32), 2) + lax.rem(part + tx + tz, 2)
         return place(tx, ty, tz)
 
     def bytes_wait(buffer, sem):
         pltpu.make_async_copy(buffer, buffer, sem).wait()
 
-    def exchange_sends(u, half):
-        slot_r = (core * 8 + row) * 16 + lax.div(col, 2)
-        if u == 0:
-            slot_l = (core * 4 + lax.rem(row, 4)) * 16 + lax.div(col, 2)
-        else:
-            slot_l = (core * 8 + row) * 8 + lax.rem(lax.div(col, 2), 8)
-
-        def right(t, _):
+    def send_right(u, part):
+        slot = (core * 8 + row) * 16 + lax.div(col, 2)
+
+        def one(t, _):
             there, trow, tcol = target(t)
 
             @pl.when(there != chip)
             def _():
                 pltpu.make_async_remote_copy(
-                    send_r.at[u, there], recv_r.at[u, slot_r],
+                    send_r.at[u, there], recv_r.at[u, slot],
                     sems_send.at[u, 0], sems_recv.at[u, 0],
                     device_id=(trow, tcol + core), device_id_type=MESH,
                 ).start()
 
             return 0
 
-        def left(t, _):
+        lax.fori_loop(64 * part, 64 * part + 64, one, 0, unroll=UNROLL)
+        if part == 1:
+            recv_r[u, slot] = send_r[u, chip]
+
+    def send_left(u, half, part):
+        if u == 0:
+            slot = (core * 4 + lax.rem(row, 4)) * 16 + lax.div(col, 2)
+        else:
+            slot = (core * 8 + row) * 8 + lax.rem(lax.div(col, 2), 8)
+
+        def one(t, _):
             there, trow, tcol = target(t)
 
             @pl.when(jnp.logical_or(there != chip, core != half))
             def _():
                 pltpu.make_async_remote_copy(
-                    send_l.at[u, there], recv_l.at[u, slot_l],
+                    send_l.at[u, there], recv_l.at[u, slot],
                     sems_send.at[u, 1], sems_recv.at[u, 1],
                     device_id=(trow, tcol + half), device_id_type=MESH,
                 ).start()
 
             return 0
 
-        if SPLIT:
-            for part in range(2):
-                lax.fori_loop(64 * part, 64 * part + 64, right, 0)
-                lax.fori_loop(64 * part, 64 * part + 64, left, 0)
-        else:
-            lax.fori_loop(0, 128, right, 0)
-            lax.fori_loop(0, 128, left, 0)
-        recv_r[u, slot_r] = send_r[u, chip]
-
-        @pl.when(core == half)
-        def _():
-            recv_l[u, slot_l] = send_l[u, chip]
+        lax.fori_loop(64 * part, 64 * part + 64, one, 0, unroll=UNROLL)
+        if part == 1:
+
+            @pl.when(core == half)
+            def _():
+                recv_l[u, slot] = send_l[u, chip]
 
     def send_mixed(u):
         def one(t, _):
-            tz = lax.rem(t, 8)
-            rest = lax.div(t, 8)
-            if FAR:
-                tz = far(tz, 8)
-            tz = lax.rem(z + tz, 8)
-            if CORE_FIRST and u == 0:
-                tcore, rest = lax.div(rest, 8), lax.rem(rest, 8)
-                if FAR:
-                    rest = 7 - rest
-                txl, rest = lax.rem(xl + rest, 2), lax.div(rest, 2)
-                tlow = txl * 2 + tcore
+            if u == 0:
+                tz = lax.rem(z + far(lax.rem(lax.div(t, 8), 8), 8), 8)
+                rest = 7 - lax.rem(t, 8)
+                tlow = lax.rem(xl + rest, 2) * 2 + lax.div(t, 64)
+                trow = lax.rem(row + lax.div(rest, 2), 4)
             else:
-                if FAR:
-                    rest = 15 - rest
+                tz = lax.rem(z + far(lax.div(t, 16), 8), 8)
+                rest = 15 - lax.rem(t, 16)
                 tlow = lax.rem(low + lax.rem(rest, 4), 4)
-                rest = lax.div(rest, 4)
-            trow = lax.rem(row + rest, 4)
+                trow = lax.rem(row + lax.div(rest, 4), 4)
             tcol = tz * 4 + tlow
 
             @pl.when(jnp.logical_or(core * 4 + trow != row, tcol != col))
@@ -220,7 +203,7 @@
 
             return 0
 
-        lax.fori_loop(0, 128, one, 0)
+        lax.fori_loop(0, 128, one, 0, unroll=UNROLL)
 
         @pl.when(core == half_r)
         def _():
@@ -250,55 +233,61 @@
         lane = lax.broadcasted_iota(jnp.int32, first.shape, 2)
         low_half = jnp.where(lane < 64, first, pltpu.roll(second, 64, 2))
         high_half = jnp.where(lane < 64, pltpu.roll(first, 64, 2), second)
-        return jnp.concatenate([low_half, high_half], axis=1).astype(BF16)
+        return jnp.concatenate([low_half, high_half], axis=1)
 
     def arrange_right(u):
         for par in range(2):
             for p in range(4):
                 base = (par * 8 + 2 * p) * 16
-                a_r[:, par, :, p * 128 : (p + 1) * 128] = woven(
-                    recv_r[u, base : base + 16], recv_r[u, base + 16 : base + 32]
-                )
+                block = woven(recv_r[u, base : base + 16], recv_r[u, base + 16 : base + 32])
+                if u == 0:
+                    a_rt[p * 128 : (p + 1) * 128, par * 256 : (par + 1) * 256] = jnp.transpose(
+                        block.reshape(256, 128)
+                    ).astype(BF16)
+                else:
+                    a_r[:, par, :, p * 128 : (p + 1) * 128] = block.astype(BF16)
 
     def arrange_left(u):
         for par in range(2):
             if u == 0:
                 for p in range(2):
                     base = (par * 4 + 2 * p) * 16
-                    a_l0[:, par, :, p * 128 : (p + 1) * 128] = woven(
+                    a_l0[par, :, :, p * 128 : (p + 1) * 128] = woven(
                         recv_l[u, base : base + 16], recv_l[u, base + 16 : base + 32]
-                    )
+                    ).astype(BF16)
             else:
                 for p in range(4):
                     base = (par * 8 + 2 * p) * 8
                     a_l1[:, par, :, p * 128 : (p + 1) * 128] = woven(
                         recv_l[u, base : base + 8], recv_l[u, base + 8 : base + 16]
-                    )
+                    ).astype(BF16)
 
     def contract(u):
-        right = a_r[...].reshape(512, 512)
-        if u == 0:
-            left = a_l0[...].reshape(512, 256)
-            mixed[...] = lax.dot_general(
-                right, left, (((0,), (0,)), ((), ())), preferred_element_type=F32
-            )
-        else:
-            left = a_l1[...].reshape(256, 512)
-            mixed[...] = lax.dot_general(
-                right, left, (((1,), (1,)), ((), ())), preferred_element_type=F32
-            )
-
-    def pack_mixed(u):
-        for p in range(2):
-            both = mixed[:, p * 128 : (p + 1) * 128].reshape(32, 2, 8, 128)
-            low_rows, high_rows = both[:, 0], both[:, 1]
-            lane = lax.broadcasted_iota(jnp.int32, low_rows.shape, 2)
-            send_m[u, 64 * p : 64 * p + 32] = jnp.where(
-                lane < 64, low_rows, pltpu.roll(high_rows, 64, 2)
-            ).astype(BF16)
-            send_m[u, 64 * p + 32 : 64 * p + 64] = jnp.where(
-                lane < 64, pltpu.roll(low_rows, 64, 2), high_rows
-            ).astype(BF16)
+        for m in range(4):
+            if u == 0:
+                mixed = jnp.dot(
+                    a_rt[128 * m : 128 * m + 128, :],
+                    a_l0[...].reshape(512, 256),
+                    preferred_element_type=F32,
+                )
+            else:
+                mixed = lax.dot_general(
+                    a_r[4 * m : 4 * m + 4].reshape(128, 512),
+                    a_l1[...].reshape(256, 512),
+                    (((1,), (1,)), ((), ())),
+                    preferred_element_type=F32,
+                )
+            for p in range(2):
+                both = mixed[:, p * 128 : (p + 1) * 128].reshape(8, 2, 8, 128)
+                low_rows, high_rows = both[:, 0], both[:, 1]
+                lane = lax.broadcasted_iota(jnp.int32, low_rows.shape, 2)
+                start = 64 * p + 8 * m
+                send_m[u, start : start + 8] = jnp.where(
+                    lane < 64, low_rows, pltpu.roll(high_rows, 64, 2)
+                ).astype(BF16)
+                send_m[u, start + 32 : start + 40] = jnp.where(
+                    lane < 64, pltpu.roll(low_rows, 64, 2), high_rows
+                ).astype(BF16)
 
     def widen_mixed(u):
         def put(n, _):
@@ -318,8 +307,12 @@
         return state[n] + gates[n] * outcome
 
     def exchange(u, half, cover):
-        pack(u)
-        exchange_sends(u, half)
+        send_right(u, 0)
+        project(u, 0, tmp_l, send_l)
+        send_left(u, half, 0)
+        send_right(u, 1)
+        send_left(u, half, 1)
+        open_gates(u)
         cover()
         shared = share_right(u)
         shared.wait_recv()
@@ -327,11 +320,21 @@
         wait_messages(recv_l.at[u], sems_recv.at[u, 1], core == half)
         arrange_left(u)
         contract(u)
-        pack_mixed(u)
         send_mixed(u)
         wait_messages(recv_m.at[u], sems_recv.at[u, 2], core == half_r)
         widen_mixed(u)
         return shared
+
+    def meet():
+        pl.semaphore_wait(barrier, 38)
+
+        def greet_again(t, _):
+            pl.semaphore_signal(
+                sem_enter, inc=1, device_id=(lax.rem(row + t, 8), col), device_id_type=MESH
+            )
+            return 0
+
+        lax.fori_loop(1, 8, greet_again, 0)
 
     for load in loads:
         load.wait()
@@ -347,17 +350,10 @@
         ]
         values = jnp.concatenate([jnp.transpose(block) for block in blocks], axis=1)
         state[n] = values
-        project(0, n, values)
-
-    pl.semaphore_wait(barrier, 38)
-
-    def greet_again(t, _):
-        pl.semaphore_signal(
-            sem_enter, inc=1, device_id=(lax.rem(row + t, 8), col), device_id_type=MESH
-        )
-        return 0
-
-    lax.fori_loop(1, 8, greet_again, 0)
+        normalise(0, n, values)
+    meet()
+    project(0, 256, tmp_r, send_r)
+
     pl.semaphore_wait(sem_enter, 7)
 
     def cover():
@@ -370,7 +366,8 @@
     for n in range(4):
         values = finish(0, n)
         state[n] = values
-        project(1, n, values)
+        normalise(1, n, values)
+    project(1, 256, tmp_r, send_r)
 
     shared1 = exchange(1, half_z, lambda: None)
 
@@ -426,10 +423,11 @@
             pltpu.VMEM((2, 128, 8, 128), BF16),
             pltpu.VMEM((2, 256, 8, 128), BF16),
             pltpu.VMEM((2, 128, 8, 128), BF16),
-            pltpu.VMEM((16, 2, 16, 256), BF16),
+            pltpu.VMEM((2, 16, 16, 256), BF16),
             pltpu.VMEM((8, 2, 16, 512), BF16),
             pltpu.VMEM((16, 2, 16, 512), BF16),
-            pltpu.VMEM((512, 256), F32),
+            pltpu.VMEM((512, 512), BF16),
+            pltpu.VMEM((4, 128, 256), BF16),
             pltpu.SemaphoreType.DMA((2, 4)),
             pltpu.SemaphoreType.DMA((2, 4)),
             pltpu.SemaphoreType.REGULAR,

time: 71.7 us -> 67.9 us (0.947)
  Pallas kernels: 69.7 us -> 65.9 us
    pallas_call x1, Pallas kernels: 69.7 us -> 65.9 us  [body(): pl.pallas_call(kernel, out_shape=jax.ShapeDtypeStruct((1024, 128), F32),...]
where the time goes in v4:
time: 67.9 us; the launch traced here: 67.8 us
  Pallas kernels  65.9 us (97%)
  local copies, waits for them, and re-layouts  1.87 us (3%)
    pallas_call x1, Pallas kernels, body(): pl.pallas_call(kernel, out_shape=jax.ShapeDtypeStruct((1024, 128), F32),...  65.9 us
    unnamed x1, local copies, waits for them, and re-layouts  1.87 us

profile of v4, /device:TPU:1, one launch (start us, length us, event | category | flops | bytes accessed | tf_op | source)
XLA Modules:
  0.0 67.8 jit_solution(4742604843696543884)
XLA Ops:
  0.0 65.9 %shard_map.91 = f32[1024,128]{1,0:T(8,128)} custom-call(f32[1024,128]{1,0:T(8,128)} %bitcast.3, f32[2,128]{1,0:T(2,128)} %in_gain_in.1, f32[2,128]{1,0:T(2,128)} %in_bias_in.1, bf16[2,128,640]{2,1,0:T(8,128)(2,1)} %proj_w_in.1, f32[2,640]{1,0:T(2,128)} %proj_b_in.1, f32[2,128]{1,0:T(2,128)} %mid_gain_in.1, f32[2,128]{1,0:T(2,128)} %mid_bias_in.1, ...), custom_call_target="tpu_custom_call" | custom-call | tf_op jit(solution)/shard_map/pallas_call | solution.py:391
  65.9 1.9 %copy.11 = f32[64,16,128]{2,1,0:T(8,128)} copy(f32[64,16,128]{2,1,0:T(8,128)} %bitcast.2) | data formatting | bytes 1048576

commit v5 on v4

--- a/solution.py
+++ b/solution.py
@@ -180,17 +180,7 @@
                 recv_l[u, slot] = send_l[u, chip]
 
     def send_mixed(u):
-        def one(t, _):
-            if u == 0:
-                tz = lax.rem(z + far(lax.rem(lax.div(t, 8), 8), 8), 8)
-                rest = 7 - lax.rem(t, 8)
-                tlow = lax.rem(xl + rest, 2) * 2 + lax.div(t, 64)
-                trow = lax.rem(row + lax.div(rest, 2), 4)
-            else:
-                tz = lax.rem(z + far(lax.div(t, 16), 8), 8)
-                rest = 15 - lax.rem(t, 16)
-                tlow = lax.rem(low + lax.rem(rest, 4), 4)
-                trow = lax.rem(row + lax.div(rest, 4), 4)
+        def to(tz, tlow, trow):
             tcol = tz * 4 + tlow
 
             @pl.when(jnp.logical_or(core * 4 + trow != row, tcol != col))
@@ -201,9 +191,27 @@
                     device_id=(core * 4 + trow, tcol), device_id_type=MESH,
                 ).start()
 
-            return 0
-
-        lax.fori_loop(0, 128, one, 0, unroll=UNROLL)
+        def some(m, tcore):
+            def one(t, _):
+                tz = 2 * m + lax.div(t, 8 if u == 0 else 16)
+                if u == 0:
+                    rest = 7 - lax.rem(t, 8)
+                    to(tz, lax.rem(xl + rest, 2) * 2 + tcore, lax.rem(row + lax.div(rest, 2), 4))
+                else:
+                    rest = 15 - lax.rem(t, 16)
+                    to(tz, lax.rem(low + lax.rem(rest, 4), 4), lax.rem(row + lax.div(rest, 4), 4))
+                return 0
+
+            lax.fori_loop(0, 16 if u == 0 else 32, one, 0, unroll=UNROLL)
+
+        blocks = [lax.rem(lax.div(z, 2) + ahead, 4) for ahead in (2, 1, 3, 0)]
+        for n in range(4):
+            contract(u, blocks[n])
+        for n in range(4):
+            some(blocks[n], 0)
+        if u == 0:
+            for n in range(4):
+                some(blocks[n], 1)
 
         @pl.when(core == half_r)
         def _():
@@ -262,32 +270,31 @@
                         recv_l[u, base : base + 8], recv_l[u, base + 8 : base + 16]
                     ).astype(BF16)
 
-    def contract(u):
-        for m in range(4):
-            if u == 0:
-                mixed = jnp.dot(
-                    a_rt[128 * m : 128 * m + 128, :],
-                    a_l0[...].reshape(512, 256),
-                    preferred_element_type=F32,
-                )
-            else:
-                mixed = lax.dot_general(
-                    a_r[4 * m : 4 * m + 4].reshape(128, 512),
-                    a_l1[...].reshape(256, 512),
-                    (((1,), (1,)), ((), ())),
-                    preferred_element_type=F32,
-                )
-            for p in range(2):
-                both = mixed[:, p * 128 : (p + 1) * 128].reshape(8, 2, 8, 128)
-                low_rows, high_rows = both[:, 0], both[:, 1]
-                lane = lax.broadcasted_iota(jnp.int32, low_rows.shape, 2)
-                start = 64 * p + 8 * m
-                send_m[u, start : start + 8] = jnp.where(
-                    lane < 64, low_rows, pltpu.roll(high_rows, 64, 2)
-                ).astype(BF16)
-                send_m[u, start + 32 : start + 40] = jnp.where(
-                    lane < 64, pltpu.roll(low_rows, 64, 2), high_rows
-                ).astype(BF16)
+    def contract(u, m):
+        if u == 0:
+            mixed = jnp.dot(
+                a_rt[pl.ds(pl.multiple_of(128 * m, 128), 128), :],
+                a_l0[...].reshape(512, 256),
+                preferred_element_type=F32,
+            )
+        else:
+            mixed = lax.dot_general(
+                a_r[pl.ds(4 * m, 4)].reshape(128, 512),
+                a_l1[...].reshape(256, 512),
+                (((1,), (1,)), ((), ())),
+                preferred_element_type=F32,
+            )
+        for p in range(2):
+            both = mixed[:, p * 128 : (p + 1) * 128].reshape(8, 2, 8, 128)
+            low_rows, high_rows = both[:, 0], both[:, 1]
+            lane = lax.broadcasted_iota(jnp.int32, low_rows.shape, 2)
+            start = 64 * p + 8 * m
+            send_m[u, pl.ds(start, 8)] = jnp.where(
+                lane < 64, low_rows, pltpu.roll(high_rows, 64, 2)
+            ).astype(BF16)
+            send_m[u, pl.ds(start + 32, 8)] = jnp.where(
+                lane < 64, pltpu.roll(low_rows, 64, 2), high_rows
+            ).astype(BF16)
 
     def widen_mixed(u):
         def put(n, _):
@@ -319,7 +326,6 @@
         arrange_right(u)
         wait_messages(recv_l.at[u], sems_recv.at[u, 1], core == half)
         arrange_left(u)
-        contract(u)
         send_mixed(u)
         wait_messages(recv_m.at[u], sems_recv.at[u, 2], core == half_r)
         widen_mixed(u)

time: 67.9 us -> 67.5 us (level)
  no operation moved by 1% of the time
where the time goes in v5:
time: 67.5 us; the launch traced here: 67.4 us
  Pallas kernels  65.5 us (97%)
  local copies, waits for them, and re-layouts  1.87 us (3%)
    pallas_call x1, Pallas kernels, body(): pl.pallas_call(kernel, out_shape=jax.ShapeDtypeStruct((1024, 128), F32),...  65.5 us
    unnamed x1, local copies, waits for them, and re-layouts  1.87 us

profile of v5, /device:TPU:1, one launch (start us, length us, event | category | flops | bytes accessed | tf_op | source)
XLA Modules:
  0.0 67.4 jit_solution(3914830049868490434)
XLA Ops:
  0.0 65.5 %shard_map.91 = f32[1024,128]{1,0:T(8,128)} custom-call(f32[1024,128]{1,0:T(8,128)} %bitcast.3, f32[2,128]{1,0:T(2,128)} %in_gain_in.1, f32[2,128]{1,0:T(2,128)} %in_bias_in.1, bf16[2,128,640]{2,1,0:T(8,128)(2,1)} %proj_w_in.1, f32[2,640]{1,0:T(2,128)} %proj_b_in.1, f32[2,128]{1,0:T(2,128)} %mid_gain_in.1, f32[2,128]{1,0:T(2,128)} %mid_bias_in.1, ...), custom_call_target="tpu_custom_call" | custom-call | tf_op jit(solution)/shard_map/pallas_call | solution.py:397
  65.5 1.9 %copy.11 = f32[64,16,128]{2,1,0:T(8,128)} copy(f32[64,16,128]{2,1,0:T(8,128)} %bitcast.2) | data formatting | bytes 1048576

commit v6 on v5

--- a/solution.py
+++ b/solution.py
@@ -191,8 +191,13 @@
                     device_id=(core * 4 + trow, tcol), device_id_type=MESH,
                 ).start()
 
-        def some(m, tcore):
+        def some(first, second, tcore):
             def one(t, _):
+                if second is None:
+                    m = first
+                else:
+                    m = lax.select(lax.rem(t, 2) == 0, first, second)
+                    t = lax.div(t, 2)
                 tz = 2 * m + lax.div(t, 8 if u == 0 else 16)
                 if u == 0:
                     rest = 7 - lax.rem(t, 8)
@@ -202,16 +207,20 @@
                     to(tz, lax.rem(low + lax.rem(rest, 4), 4), lax.rem(row + lax.div(rest, 4), 4))
                 return 0
 
-            lax.fori_loop(0, 16 if u == 0 else 32, one, 0, unroll=UNROLL)
+            count = (16 if u == 0 else 32) * (1 if second is None else 2)
+            lax.fori_loop(0, count, one, 0, unroll=UNROLL)
+
+        def all_blocks(tcore):
+            some(blocks[0], None, tcore)
+            some(blocks[1], blocks[2], tcore)
+            some(blocks[3], None, tcore)
 
         blocks = [lax.rem(lax.div(z, 2) + ahead, 4) for ahead in (2, 1, 3, 0)]
         for n in range(4):
             contract(u, blocks[n])
-        for n in range(4):
-            some(blocks[n], 0)
+        all_blocks(0)
         if u == 0:
-            for n in range(4):
-                some(blocks[n], 1)
+            all_blocks(1)
 
         @pl.when(core == half_r)
         def _():

time: 67.5 us -> 67.6 us (level)
  no operation moved by 1% of the time
where the time goes in v6:
time: 67.6 us; the launch traced here: 67.4 us
  Pallas kernels  65.5 us (97%)
  local copies, waits for them, and re-layouts  1.87 us (3%)
    pallas_call x1, Pallas kernels, body(): pl.pallas_call(kernel, out_shape=jax.ShapeDtypeStruct((1024, 128), F32),...  65.5 us
    unnamed x1, local copies, waits for them, and re-layouts  1.87 us

profile of v6, /device:TPU:1, one launch (start us, length us, event | category | flops | bytes accessed | tf_op | source)
XLA Modules:
  0.0 67.4 jit_solution(16458891186795624288)
XLA Ops:
  0.0 65.5 %shard_map.91 = f32[1024,128]{1,0:T(8,128)} custom-call(f32[1024,128]{1,0:T(8,128)} %bitcast.3, f32[2,128]{1,0:T(2,128)} %in_gain_in.1, f32[2,128]{1,0:T(2,128)} %in_bias_in.1, bf16[2,128,640]{2,1,0:T(8,128)(2,1)} %proj_w_in.1, f32[2,640]{1,0:T(2,128)} %proj_b_in.1, f32[2,128]{1,0:T(2,128)} %mid_gain_in.1, f32[2,128]{1,0:T(2,128)} %mid_bias_in.1, ...), custom_call_target="tpu_custom_call" | custom-call | tf_op jit(solution)/shard_map/pallas_call | solution.py:406
  65.5 1.9 %copy.11 = f32[64,16,128]{2,1,0:T(8,128)} copy(f32[64,16,128]{2,1,0:T(8,128)} %bitcast.2) | data formatting | bytes 1048576
